TPU v7x, 256 devices: a whole 4x4x8 slice. The times are simulated.
256 devices in a mesh: grp: 32 (over y, z_lo, core), dev: 8 (over x, z_hi).
Axes of the slice: x: 4, y: 4, z: 8 (z_hi: 2, z_lo: 4; z = z_hi * 4 + z_lo), core: 2. Of those that a mesh axis runs over, the one named last changes fastest.
Arguments:
- stack: bfloat16 [608, 256, 2048], P('grp', None, 'dev'), may hold values from -12 to 12
- network: int32 [608, 2], replicated, may hold values from 0 to 149, as said below
- bands: int32 [149], replicated, may hold values from 1 to 8
Outputs:
- deramped: bfloat16 [149, 256, 2048], P(None, 'grp', 'dev')
- misfit: float32 [256, 2048], P('grp', 'dev')
- spectrum: float32 [2, 149, 15, 15], replicated
Inputs may be any that keep to these rules, and one draw needn't show every extreme that they name: `network`: each row holds a reference date and a later secondary date, both below 150; every pair of consecutive dates is some row.
All inputs are finite; a program needn't handle non-finite values.
Results may differ from a plain program's by a relative error of at most 0.005.
Values may be sent and summed in bfloat16 or wider, within the bound.
No kernel may reach another device: no remote copies, remote signals or barrier semaphores. Data moves between devices by JAX's collectives and lax.ppermute only.
A program may use at most 128 MiB of HBM per device.

v0:
```python
import math
import jax
import jax.numpy as jnp
import numpy as np
from jax import lax
from jax.sharding import PartitionSpec as P

BAND = 8
FREQS = 2 * BAND - 1
HIGH = lax.Precision.HIGHEST


def design_of(network, solved):
    dates = jnp.arange(1, solved + 1, dtype=jnp.int32)
    return (network[:, 1:2] == dates[None, :]).astype(jnp.float32) - (
        network[:, 0:1] == dates[None, :]
    ).astype(jnp.float32)


def build_inverse(network, solved):
    design = design_of(network, solved)
    normal = jnp.dot(design.T, design, precision=HIGH)
    factor = jnp.linalg.cholesky(normal)
    pinv = jax.scipy.linalg.cho_solve((factor, True), design.T)
    return (pinv.astype(jnp.bfloat16), design.astype(jnp.bfloat16))


def basis(positions, length):
    index = jnp.arange(FREQS, dtype=jnp.int32)
    step = jnp.where(index < BAND, index, index - (BAND - 1))
    turns = positions[:, None] * step[None, :] % length
    angle = turns.astype(jnp.float32) * (2.0 * math.pi / length)
    return jnp.where(index[None, :] < BAND, jnp.cos(angle), jnp.sin(angle))


def mirror():
    out = np.zeros((FREQS, FREQS, 2, FREQS, FREQS), np.float32)
    for k in range(FREQS):
        for l in range(FREQS):
            fk, fl = (k - (BAND - 1), l - (BAND - 1))
            ck, cl = (abs(fk), abs(fl))
            sk, sl = (abs(fk) + BAND - 1, abs(fl) + BAND - 1)
            gk, gl = (np.sign(fk), np.sign(fl))
            out[k, l, 0, ck, cl] += 1
            if gk * gl:
                out[k, l, 0, sk, sl] -= gk * gl
            if gk:
                out[k, l, 1, sk, cl] -= gk
            if gl:
                out[k, l, 1, ck, sl] -= gl
    return out.reshape(FREQS * FREQS * 2, FREQS * FREQS)


def on_device(stack, network, bands):
    solved = bands.shape[0]
    groups = lax.axis_size("grp")
    held, rows_all, col_dev = stack.shape
    row_dev = rows_all // groups
    cols_all = col_dev * lax.axis_size("dev")
    pixels = row_dev * col_dev
    packed = stack.reshape(held, groups, row_dev, col_dev).transpose(1, 0, 2, 3)
    block = lax.all_to_all(packed, "grp", 0, 0, tiled=True)
    rows = basis(jnp.arange(rows_all, dtype=jnp.int32), rows_all)
    cols = basis(lax.axis_index("dev") * col_dev + jnp.arange(col_dev, dtype=jnp.int32), cols_all)
    wide = stack.astype(jnp.float32)
    half = jnp.einsum("ihw,ha->iaw", wide, rows, precision=HIGH)
    local = jnp.einsum("iaw,wb->iab", half, cols, precision=HIGH)
    local = local.reshape(held, FREQS * FREQS)
    summed = lax.psum(local, "dev")
    every = lax.all_gather(summed, "grp", axis=0, tiled=True)
    pinv, design = build_inverse(network, solved)
    scale = 1.0 / (rows_all * cols_all)
    coef = scale * lax.dot_general(
        every, pinv.astype(jnp.float32), (((0,), (1,)), ((), ())), precision=HIGH
    )
    index = np.arange(FREQS)
    step = np.where(index < BAND, index, index - (BAND - 1))
    weight = np.where(step == 0, 1.0, 2.0)
    kmax = np.maximum(step[:, None], step[None, :]).reshape(-1)
    both = (weight[:, None] * weight[None, :]).reshape(-1).astype(np.float32)
    masked = jnp.where(jnp.asarray(kmax)[:, None] < bands[None, :], coef, 0.0)
    signed = jnp.dot(jnp.asarray(mirror()), masked, precision=HIGH)
    spectrum = signed.reshape(FREQS, FREQS, 2, solved).transpose(2, 3, 0, 1)
    row_here = basis(
        lax.axis_index("grp") * row_dev + jnp.arange(row_dev, dtype=jnp.int32), rows_all
    )
    waves = (row_here.T[:, None, :, None] * cols.T[None, :, None, :]).reshape(FREQS * FREQS, pixels)
    ramp = lax.dot_general(
        masked * jnp.asarray(both)[:, None], waves, (((0,), (0,)), ((), ())), precision=HIGH
    )
    flat = block.reshape(held * groups, pixels)
    series = jnp.dot(pinv, flat, preferred_element_type=jnp.float32)
    deramped = (series - ramp).astype(jnp.bfloat16).reshape(solved, row_dev, col_dev)
    model = jnp.dot(design, series.astype(jnp.bfloat16), preferred_element_type=jnp.float32)
    resid = flat.astype(jnp.float32) - model
    misfit = jnp.sqrt(jnp.mean(resid * resid, axis=0) + 1e-06).reshape(row_dev, col_dev)
    return (deramped, misfit, spectrum)


def solution(mesh):
    return jax.shard_map(
        on_device,
        mesh=mesh,
        in_specs=(P("grp", None, "dev"), P(), P()),
        out_specs=(P(None, "grp", "dev"), P("grp", "dev"), P()),
        check_vma=False,
    )
```

profile of v0, /device:TPU:1, one launch (start us, length us, event | category | flops | bytes accessed | tf_op | source)
XLA Modules:
  0.0 182.2 jit_solution(6894326143020125078)
XLA Ops:
  0.6 1.7 copy-done
  2.3 1.6 copy_bitcast_fusion
  4.0 10.4 %all-to-all-start = ((bf16[32,19,8,256]{3,2,1,0:T(8,128)(2,1)}), bf16[32,19,8,256]{3,2,1,0:T(8,128)(2,1)}, u32[]{:S(2)}, u32[]{:S(2)}) async-start(bf16[32,19,8,256]{3,2,1,0:T(8,128)(2,1)} %copy_bitcast_fusion), calls=%async_computation | async-start | bytes 4980736 | tf_op jit(solution)/shard_map/all_to_all | solution.py:62
  14.4 1.5 fusion.4
  16.1 11.7 %cholesky.51 = f32[128,128]{1,0:T(8,128)S(1)} custom-call(f32[128,128]{1,0:T(8,128)S(1)} %cholesky.124), custom_call_target="Cholesky" | custom-call | tf_op jit(solution)/shard_map/jit(cholesky)/cholesky | solution.py:23
  27.8 9.8 %custom-call.18 = f32[1,128,128]{1,2,0:T(8,128)S(1)} custom-call(f32[1,128,128]{2,1,0:T(8,128)S(1)} %get-tuple-element.26), custom_call_target="InvertDiagBlocksLowerTriangular" | custom-call | tf_op jit(solution)/shard_map/jit(cholesky)/cholesky | solution.py:23
  38.0 1.9 %cholesky.110 = f32[21,21]{1,0:T(8,128)S(1)} custom-call(f32[21,21]{1,0:T(8,128)S(1)} %convolution_subtract_fusion.3), custom_call_target="Cholesky" | custom-call | tf_op jit(solution)/shard_map/jit(cholesky)/cholesky | solution.py:23
  39.9 0.6 compare_reduce_fusion
  40.6 0.6 compare_reduce_fusion.1
  42.7 19.9 %custom-call.19 = f32[2,128,128]{1,2,0:T(8,128)S(1)} custom-call(f32[2,128,128]{2,1,0:T(8,128)S(1)} %pad_maximum_fusion.3), custom_call_target="InvertDiagBlocksLowerTriangular" | custom-call | tf_op jit(solution)/shard_map/jit(_cho_solve)/triangular_solve | solution.py:24
  62.7 0.7 fusion.7
  63.4 0.7 copy-done.2
  64.2 0.4 convolution_subtract_fusion.2
  64.6 0.3 fusion.53
  65.3 1.2 convolution_bitcast_fusion
  66.5 0.5 fusion.32
  67.1 45.8 %psum.7 = f32[19,225]{1,0:T(8,128)S(1)} all-reduce(f32[19,225]{1,0:T(8,128)S(1)} %reshape.205), channel_id=1, replica_groups=mesh['grp'=32,'dev'=8] {'dev'}, use_global_device_ids=true, to_apply=%region_4.5 | all-reduce | flops 4275 | bytes 34200 | tf_op jit(solution)/shard_map/psum | solution.py:69
  112.9 53.9 %all-gather = f32[32,19,225]{2,1,0:T(8,128)S(1)} all-gather(f32[1,19,225]{2,1,0:T(8,128)S(1)} %bitcast.72), channel_id=1, replica_groups=mesh['grp'=32,'dev'=8] {'grp'}, dimensions={0}, use_global_device_ids=true | all-gather | bytes 564300 | tf_op jit(solution)/shard_map/all_gather | solution.py:70
  166.8 0.9 reshape.238
  168.4 2.1 %copy.23 = f32[29,8,8,256]{3,1,2,0:T(8,128)} copy(f32[29,8,8,256]{3,2,1,0:T(8,128)S(1)} %bitcast.67) | data formatting | bytes 3801088
  170.5 1.4 convolution_subtract_fusion.1
  171.9 0.4 convolution_convert_fusion
  172.3 0.5 fusion.1
  172.9 0.5 fusion.83
  173.4 1.0 reshape.207
  174.5 2.5 %copy.22 = bf16[76,8,8,256]{3,1,2,0:T(8,128)(2,1)S(1)} copy(bf16[76,8,8,256]{3,2,1,0:T(8,128)(2,1)} %bitcast.15) | data formatting | bytes 4980736
  177.0 0.7 fusion.16
  177.7 1.0 multiply_reduce_fusion
  178.7 0.5 copy-done.1
  179.2 1.3 fusion
  180.7 0.9 slice.94
  181.6 0.6 sqrt.8
  (54 shorter events, 2.1 us)
Async XLA Ops:
  0.6 1.7 copy-start
  4.0 10.4 %copy-start.9 = (s32[608,2]{0,1:T(2,128)S(1)}, s32[608,2]{0,1:T(2,128)}, u32[]{:S(2)}) copy-start(s32[608,2]{0,1:T(2,128)} %param.7) | copy-start | bytes 14596
  4.0 170.5 %all-to-all-start = ((bf16[32,19,8,256]{3,2,1,0:T(8,128)(2,1)}), bf16[32,19,8,256]{3,2,1,0:T(8,128)(2,1)}, u32[]{:S(2)}, u32[]{:S(2)}) async-start(bf16[32,19,8,256]{3,2,1,0:T(8,128)(2,1)} %copy_bitcast_fusion), calls=%async_computation | async-start | bytes 4980736 | tf_op jit(solution)/shard_map/all_to_all | solution.py:62
  42.5 23.9 %copy-start.6 = (f32[149,149]{1,0:T(8,128)}, f32[149,149]{1,0:T(8,128)S(1)}, u32[]{:S(2)}) copy-start(f32[149,149]{1,0:T(8,128)S(1)} %select_select_fusion) | copy-start | bytes 266416
  62.6 2.7 %copy-start.7 = (f32[2,128,128]{1,2,0:T(8,128)}, f32[2,128,128]{1,2,0:T(8,128)S(1)}, u32[]{:S(2)}) copy-start(f32[2,128,128]{1,2,0:T(8,128)S(1)} %custom-call.19) | copy-start | bytes 393220
  63.4 0.7 copy-start.2
  168.3 2.2 %copy-start.3 = (f32[128,608]{0,1:T(8,128)S(1)}, f32[128,608]{0,1:T(8,128)}, u32[]{:S(2)}) copy-start(f32[128,608]{0,1:T(8,128)} %copy-done.2) | copy-start | bytes 933892
  168.3 3.5 %copy-start.8 = (f32[2,128,128]{1,2,0:T(8,128)S(1)}, f32[2,128,128]{1,2,0:T(8,128)}, u32[]{:S(2)}) copy-start(f32[2,128,128]{1,2,0:T(8,128)} %copy-done.7) | copy-start | bytes 393220
  168.4 4.0 %copy-start.4 = (f32[608,225]{1,0:T(8,128)S(1)}, f32[608,225]{1,0:T(8,128)}, u32[]{:S(2)}) copy-start(f32[608,225]{1,0:T(8,128)} %reshape.238) | copy-start | bytes 1641604
  168.4 4.0 %copy-start.11 = (s32[149]{0:T(256)S(1)}, s32[149]{0:T(256)}, u32[]{:S(2)}) copy-start(s32[149]{0:T(256)} %param.8) | copy-start | bytes 1792
  168.4 4.0 %copy-start.12 = (s32[225]{0:T(256)S(1)}, s32[225]{0:T(256)}, u32[]{:S(2)}) copy-start(s32[225]{0:T(256)} %constant.175.clone) | copy-start | bytes 2704
  168.4 4.5 %copy-start.5 = (f32[450,225]{1,0:T(8,128)S(1)}, f32[450,225]{1,0:T(8,128)}, u32[]{:S(2)}) copy-start(f32[450,225]{1,0:T(8,128)} %constant.176.clone) | copy-start | bytes 1215004
  177.7 1.5 copy-start.1
  177.7 1.5 copy-start.10
where the time goes:
time: 183 us; the launch traced here: 182 us
  blocking collectives  99.7 us (54%)
  other arithmetic  45.4 us (25%)
  local copies, waits for them, and re-layouts  13.4 us (7%)
  matrix products  11 us (6%)
  starting transfers between devices  10.4 us (6%)
  between operations  2.38 us (1%)
    all_gather x1, blocking collectives, on_device(): every = lax.all_gather(summed, 'grp', axis=0, tiled=True)  53.9 us
    psum x1, blocking collectives, on_device(): summed = lax.psum(local, 'dev')  45.8 us
    another operation x7, other arithmetic, build_inverse(): factor = jnp.linalg.cholesky(normal)  24.8 us
    another operation x6, other arithmetic, build_inverse(): pinv = jax.scipy.linalg.cho_solve((factor, True), design.T)  20 us
    all_to_all x1, starting transfers between devices, on_device(): block = lax.all_to_all(packed, 'grp', 0, 0, tiled=True)  10.4 us
    unnamed x31, local copies, waits for them, and re-layouts  8.8 us
  transfers between devices with their start and end apart: 1, of which 0 were waited for; matrix products, arithmetic and copies ran while one was open for 32% of the time, Pallas kernels for 0%

commit v1 on v0

--- a/solution.py
+++ b/solution.py
@@ -66,7 +66,7 @@
     half = jnp.einsum("ihw,ha->iaw", wide, rows, precision=HIGH)
     local = jnp.einsum("iaw,wb->iab", half, cols, precision=HIGH)
     local = local.reshape(held, FREQS * FREQS)
-    summed = lax.psum(local, "dev")
+    summed = jnp.sum(lax.all_gather(local, "dev"), axis=0)
     every = lax.all_gather(summed, "grp", axis=0, tiled=True)
     pinv, design = build_inverse(network, solved)
     scale = 1.0 / (rows_all * cols_all)

time: 183 us -> 174 us (0.951)
  blocking collectives: 99.7 us -> 91 us
    psum x1 -> x0, blocking collectives: 45.8 us -> none  [on_device(): summed = lax.psum(local, 'dev')]
    all_gather x0 -> x1, blocking collectives: none -> 38.2 us  [on_device(): summed = jnp.sum(lax.all_gather(local, 'dev'), axis=0)]
  transfers between devices with their start and end apart: 1 -> 1, of which waited for: 0 -> 0; matrix products, arithmetic and copies ran while one was open for 32% -> 33% of each run, Pallas kernels for 0% -> 0%
where the time goes in v1:
time: 174 us
  blocking collectives  91 us (52%)
  other arithmetic  45.5 us (26%)
  local copies, waits for them, and re-layouts  13.4 us (8%)
  matrix products  11 us (6%)
  starting transfers between devices  10.4 us (6%)
  between operations  2.38 us (1%)
    all_gather x1, blocking collectives, on_device(): every = lax.all_gather(summed, 'grp', axis=0, tiled=True)  52.8 us
    all_gather x1, blocking collectives, on_device(): summed = jnp.sum(lax.all_gather(local, 'dev'), axis=0)  38.2 us
    another operation x7, other arithmetic, build_inverse(): factor = jnp.linalg.cholesky(normal)  24.8 us
    another operation x6, other arithmetic, build_inverse(): pinv = jax.scipy.linalg.cho_solve((factor, True), design.T)  20 us
    all_to_all x1, starting transfers between devices, on_device(): block = lax.all_to_all(packed, 'grp', 0, 0, tiled=True)  10.4 us
    unnamed x31, local copies, waits for them, and re-layouts  8.8 us
  transfers between devices with their start and end apart: 1, of which 0 were waited for; matrix products, arithmetic and copies ran while one was open for 33% of the time, Pallas kernels for 0%

profile of v1, /device:TPU:1, one launch (start us, length us, event | category | flops | bytes accessed | tf_op | source)
XLA Modules:
  0.0 173.5 jit_solution(6064632771752645810)
XLA Ops:
  0.6 1.7 copy-done
  2.3 1.6 copy_bitcast_fusion
  4.0 10.4 %all-to-all-start = ((bf16[32,19,8,256]{3,2,1,0:T(8,128)(2,1)}), bf16[32,19,8,256]{3,2,1,0:T(8,128)(2,1)}, u32[]{:S(2)}, u32[]{:S(2)}) async-start(bf16[32,19,8,256]{3,2,1,0:T(8,128)(2,1)} %copy_bitcast_fusion), calls=%async_computation | async-start | bytes 4980736 | tf_op jit(solution)/shard_map/all_to_all | solution.py:62
  14.4 1.5 fusion.4
  16.1 11.7 %cholesky.51 = f32[128,128]{1,0:T(8,128)S(1)} custom-call(f32[128,128]{1,0:T(8,128)S(1)} %cholesky.124), custom_call_target="Cholesky" | custom-call | tf_op jit(solution)/shard_map/jit(cholesky)/cholesky | solution.py:23
  27.8 9.8 %custom-call.18 = f32[1,128,128]{1,2,0:T(8,128)S(1)} custom-call(f32[1,128,128]{2,1,0:T(8,128)S(1)} %get-tuple-element.26), custom_call_target="InvertDiagBlocksLowerTriangular" | custom-call | tf_op jit(solution)/shard_map/jit(cholesky)/cholesky | solution.py:23
  38.0 1.9 %cholesky.110 = f32[21,21]{1,0:T(8,128)S(1)} custom-call(f32[21,21]{1,0:T(8,128)S(1)} %convolution_subtract_fusion.3), custom_call_target="Cholesky" | custom-call | tf_op jit(solution)/shard_map/jit(cholesky)/cholesky | solution.py:23
  39.9 0.6 compare_reduce_fusion
  40.6 0.6 compare_reduce_fusion.1
  42.7 19.9 %custom-call.19 = f32[2,128,128]{1,2,0:T(8,128)S(1)} custom-call(f32[2,128,128]{2,1,0:T(8,128)S(1)} %pad_maximum_fusion.3), custom_call_target="InvertDiagBlocksLowerTriangular" | custom-call | tf_op jit(solution)/shard_map/jit(_cho_solve)/triangular_solve | solution.py:24
  62.7 0.7 fusion.7
  63.4 0.7 copy-done.2
  64.2 0.4 convolution_subtract_fusion.2
  64.6 0.3 fusion.53
  65.3 1.2 convolution_bitcast_fusion
  66.5 0.5 fusion.32
  67.1 38.2 %all_gather.6 = f32[8,19,225]{2,1,0:T(8,128)S(1)} all-gather(f32[1,19,225]{2,1,0:T(8,128)S(1)} %all_gather_reshape.3), channel_id=1, replica_groups=mesh['grp'=32,'dev'=8] {'dev'}, dimensions={0}, use_global_device_ids=true | all-gather | bytes 153900 | tf_op jit(solution)/shard_map/all_gather | solution.py:69
  105.4 52.8 %all-gather = f32[32,19,225]{2,1,0:T(8,128)S(1)} all-gather(f32[1,19,225]{2,1,0:T(8,128)S(1)} %bitcast.72), channel_id=1, replica_groups=mesh['grp'=32,'dev'=8] {'grp'}, dimensions={0}, use_global_device_ids=true | all-gather | bytes 564300 | tf_op jit(solution)/shard_map/all_gather | solution.py:70
  158.2 0.9 reshape.234
  159.8 2.1 %copy.23 = f32[29,8,8,256]{3,1,2,0:T(8,128)} copy(f32[29,8,8,256]{3,2,1,0:T(8,128)S(1)} %bitcast.67) | data formatting | bytes 3801088
  161.9 1.4 convolution_subtract_fusion.1
  163.3 0.4 convolution_convert_fusion
  163.7 0.5 fusion.1
  164.2 0.5 fusion.83
  164.8 1.0 reshape.203
  165.8 2.5 %copy.22 = bf16[76,8,8,256]{3,1,2,0:T(8,128)(2,1)S(1)} copy(bf16[76,8,8,256]{3,2,1,0:T(8,128)(2,1)} %bitcast.15) | data formatting | bytes 4980736
  168.4 0.7 fusion.16
  169.1 1.0 multiply_reduce_fusion
  170.0 0.5 copy-done.1
  170.6 1.3 fusion
  172.1 0.9 slice.94
  172.9 0.6 sqrt.8
  (55 shorter events, 2.2 us)
Async XLA Ops:
  0.6 1.7 copy-start
  4.0 10.4 %copy-start.9 = (s32[608,2]{0,1:T(2,128)S(1)}, s32[608,2]{0,1:T(2,128)}, u32[]{:S(2)}) copy-start(s32[608,2]{0,1:T(2,128)} %param.7) | copy-start | bytes 14596
  4.0 161.9 %all-to-all-start = ((bf16[32,19,8,256]{3,2,1,0:T(8,128)(2,1)}), bf16[32,19,8,256]{3,2,1,0:T(8,128)(2,1)}, u32[]{:S(2)}, u32[]{:S(2)}) async-start(bf16[32,19,8,256]{3,2,1,0:T(8,128)(2,1)} %copy_bitcast_fusion), calls=%async_computation | async-start | bytes 4980736 | tf_op jit(solution)/shard_map/all_to_all | solution.py:62
  42.5 23.9 %copy-start.6 = (f32[149,149]{1,0:T(8,128)}, f32[149,149]{1,0:T(8,128)S(1)}, u32[]{:S(2)}) copy-start(f32[149,149]{1,0:T(8,128)S(1)} %select_select_fusion) | copy-start | bytes 266416
  62.6 2.7 %copy-start.7 = (f32[2,128,128]{1,2,0:T(8,128)}, f32[2,128,128]{1,2,0:T(8,128)S(1)}, u32[]{:S(2)}) copy-start(f32[2,128,128]{1,2,0:T(8,128)S(1)} %custom-call.19) | copy-start | bytes 393220
  63.4 0.7 copy-start.2
  159.7 2.2 %copy-start.3 = (f32[128,608]{0,1:T(8,128)S(1)}, f32[128,608]{0,1:T(8,128)}, u32[]{:S(2)}) copy-start(f32[128,608]{0,1:T(8,128)} %copy-done.2) | copy-start | bytes 933892
  159.7 3.5 %copy-start.8 = (f32[2,128,128]{1,2,0:T(8,128)S(1)}, f32[2,128,128]{1,2,0:T(8,128)}, u32[]{:S(2)}) copy-start(f32[2,128,128]{1,2,0:T(8,128)} %copy-done.7) | copy-start | bytes 393220
  159.7 4.0 %copy-start.4 = (f32[608,225]{1,0:T(8,128)S(1)}, f32[608,225]{1,0:T(8,128)}, u32[]{:S(2)}) copy-start(f32[608,225]{1,0:T(8,128)} %reshape.234) | copy-start | bytes 1641604
  159.7 4.0 %copy-start.11 = (s32[149]{0:T(256)S(1)}, s32[149]{0:T(256)}, u32[]{:S(2)}) copy-start(s32[149]{0:T(256)} %param.8) | copy-start | bytes 1792
  159.7 4.0 %copy-start.12 = (s32[225]{0:T(256)S(1)}, s32[225]{0:T(256)}, u32[]{:S(2)}) copy-start(s32[225]{0:T(256)} %constant.175.clone) | copy-start | bytes 2704
  159.7 4.5 %copy-start.5 = (f32[450,225]{1,0:T(8,128)S(1)}, f32[450,225]{1,0:T(8,128)}, u32[]{:S(2)}) copy-start(f32[450,225]{1,0:T(8,128)} %constant.176.clone) | copy-start | bytes 1215004
  169.1 1.5 copy-start.1
  169.1 1.5 copy-start.10
